TPU v7x, 32 devices: a whole 2x2x4 slice. The times are simulated.
32 devices in a mesh: site: 4 (over z), py: 2 (over x), px: 2 (over y), pz: 2 (over core).
Axes of the slice: x: 2, y: 2, z: 4, core: 2. Of those that a mesh axis runs over, the one named last changes fastest.
Arguments:
- initial_heat_state: float32 [32, 128, 64, 128], P(('site', 'py'), 'px', 'pz'), parts along dimension 0, may hold values from 0.2 to 1.8
- scaled_speed_north: float32 [32, 128, 64, 128], P(('site', 'py'), 'px', 'pz'), parts along dimension 0, may hold values from -0.3 to 0.3
- scaled_speed_east: float32 [32, 128, 64, 128], P(('site', 'py'), 'px', 'pz'), parts along dimension 0, may hold values from -0.3 to 0.3
- scaled_speed_upward: float32 [32, 128, 64, 128], P(('site', 'py'), 'px', 'pz'), parts along dimension 0, may hold values from -0.3 to 0.3
Outputs:
- temperature_end: float32 [32, 128, 64, 128], P(('site', 'py'), 'px', 'pz'), parts along dimension 0
There are 4 independent parts, one for each index of `site`. A program takes and returns all parts, laid end to end along the dimension named above; each array names one. Nothing has to cross between parts.
All inputs are finite; a program needn't handle non-finite values.
Results may differ from a plain program's by a relative error of at most 0.00002.
Values sent between devices are 32-bit elements; how exact they have to be, the bound alone decides.
A program may use at most 256 MiB of HBM per device.

v0:
```python
import functools

import jax
import jax.numpy as jnp
from jax import lax
from jax.experimental import pallas as pl
from jax.experimental.pallas import tpu as pltpu
from jax.sharding import PartitionSpec as P

STEPS = 4
CUTS = ((0, 32, 64), (0, 32, 64), (0, 32, 64), (0, 32, 56, 62, 64))
PAD = 8
MESH = pl.DeviceIdType.MESH


def pieces(rows, t):
    ends = sorted({rows * cut // 64 for cut in CUTS[t]})
    return [(a, b - a) for a, b in zip(ends, ends[1:])]


def kernel(
    counts, x, vn, ve, vu, out, s, w,
    edge_sem, load_sem, speed_sem,
    py_send, py_recv, px_send, px_recv, pz_send, pz_recv,
):
    planes, rows, depth, _ = x.shape
    parts = [pieces(rows, t) for t in range(STEPS)]
    cells = pl.ds(PAD, depth)
    speeds = (vn, ve, vu)
    outer = sorted({1, planes})
    inner_count = planes - 2
    axes = ("py", "px", "pz")
    index = {axis: lax.axis_index(axis) for axis in axes}

    def sends(axis, way):
        return index[axis] < counts[axis] - 1 if way == 0 else index[axis] > 0

    def receives(axis, way):
        return sends(axis, 1 - way)

    def target(axis, way):
        count = counts[axis]
        return {axis: lax.rem(index[axis] + (1 if way == 0 else count - 1), count)}

    def remote(src, dst, send, recv, axis, way):
        return pltpu.make_async_remote_copy(
            src_ref=src, dst_ref=dst, send_sem=send, recv_sem=recv,
            device_id=target(axis, way), device_id_type=MESH,
        )

    def py_copy(way, t, i):
        first, span = parts[t][i]
        here = pl.ds(1 + first, span)
        src = s.at[t, planes if way == 0 else 1, here, cells]
        dst = s.at[t, 0 if way == 0 else planes + 1, here, cells]
        return remote(src, dst, py_send.at[way, t], py_recv.at[way, t, i], "py", way)

    def px_copy(way, t):
        row = rows if way == 0 else 1
        inner = pl.ds(1, planes)
        src = x.at[:, row - 1] if t == 0 else s.at[t, inner, row, cells]
        dst = s.at[t, inner, 0 if way == 0 else rows + 1, cells]
        return remote(src, dst, px_send.at[way, t], px_recv.at[way, t], "px", way)

    def pz_copy(way, t):
        inner, here = pl.ds(1, planes), pl.ds(1, rows)
        first = depth - PAD if way == 0 else 0
        if t == 0:
            src = x.at[:, :, pl.ds(first, PAD)]
        else:
            src = s.at[t, inner, here, pl.ds(PAD + first, PAD)]
        dst = s.at[t, inner, here, pl.ds(0 if way == 0 else PAD + depth, PAD)]
        return remote(src, dst, pz_send.at[way, t], pz_recv.at[way, t], "pz", way)

    def wait_sent(t):
        def py_wait(way):
            block = s.at[t, planes if way == 0 else 1, pl.ds(1, rows), cells]
            remote(block, block, py_send.at[way, t], py_recv.at[way, t, 0], "py", way).wait_send()

        each("py", sends, py_wait)
        each("pz", sends, lambda way: pz_copy(way, t).wait_send())
        each("px", sends, lambda way: px_copy(way, t).wait_send())

    def each(axis, test, action):
        if counts[axis] > 1:
            for way in (0, 1):
                pl.when(test(axis, way))(functools.partial(action, way))

    def send_py(t, i):
        each("py", sends, lambda way: py_copy(way, t, i).start())

    def send_rest(t):
        each("px", sends, lambda way: px_copy(way, t).start())
        each("pz", sends, lambda way: pz_copy(way, t).start())

    def wait_py(t, i):
        each("py", receives, lambda way: py_copy(way, t, i).wait_recv())

    def wait_rest(t):
        each("px", receives, lambda way: px_copy(way, t).wait_recv())
        each("pz", receives, lambda way: pz_copy(way, t).wait_recv())

    def speed_copy(k, i):
        here = pl.ds(*parts[0][i])
        return pltpu.make_async_copy(speeds[k].at[:, here], w.at[k, :, here], speed_sem.at[i])

    def wait_speeds(i):
        block = w.at[:, :, pl.ds(*parts[0][i])]
        pltpu.make_async_copy(block, block, speed_sem.at[i]).wait()

    def edge_load(k, i):
        first, span = parts[0][i]
        return pltpu.make_async_copy(
            x.at[outer[k] - 1, pl.ds(first, span)],
            s.at[0, outer[k], pl.ds(1 + first, span), cells],
            edge_sem.at[k, i],
        )

    barrier = pltpu.get_barrier_semaphore()
    greeted = 0
    for axis in axes:
        each(axis, sends, lambda way, axis=axis: pl.semaphore_signal(
            barrier, inc=1, device_id=target(axis, way), device_id_type=MESH))
        if counts[axis] > 1:
            for way in (0, 1):
                greeted = greeted + sends(axis, way).astype(jnp.int32)
    for i in range(len(parts[0])):
        for k in range(len(outer)):
            edge_load(k, i).start()
    if inner_count > 0:
        load = pltpu.make_async_copy(
            x.at[pl.ds(1, inner_count)],
            s.at[0, pl.ds(2, inner_count), pl.ds(1, rows), cells],
            load_sem,
        )
        load.start()

    pl.semaphore_wait(barrier, greeted)

    for i in range(len(parts[0])):
        for k in range(len(outer)):
            edge_load(k, i).wait()
        send_py(0, i)
    send_rest(0)
    for i in range(len(parts[0])):
        for k in range(3):
            speed_copy(k, i).start()

    def clear(axis, way):
        lanes = s.shape[-1]

        def fill(t, _):
            if axis == "py":
                plane = 0 if way == 0 else planes + 1

                def row_fill(r, _):
                    s[t, plane, 1 + r, PAD:PAD + depth, :] = jnp.zeros((depth, lanes), s.dtype)
                    return None

                lax.fori_loop(0, rows, row_fill, None)
            elif axis == "px":
                row = 0 if way == 0 else rows + 1
                for p in range(1, planes + 1):
                    s[t, p, row, PAD:PAD + depth, :] = jnp.zeros((depth, lanes), s.dtype)
            else:
                first = 0 if way == 0 else PAD + depth

                def row_fill(r, _):
                    for p in range(1, planes + 1):
                        s[t, p, 1 + r, first:first + PAD, :] = jnp.zeros((PAD, lanes), s.dtype)
                    return None

                lax.fori_loop(0, rows, row_fill, None)
            return None

        lax.fori_loop(0, STEPS, fill, None)

    for axis in axes:
        for way in (0, 1):
            pl.when(jnp.logical_not(receives(axis, way)))(functools.partial(clear, axis, way))

    if inner_count > 0:
        load.wait()

    def update(t, piece, wanted):
        def row(r, _):
            for z in range(PAD, PAD + depth, 8):
                here = slice(z, z + 8)
                column = {}
                for p in wanted:
                    for q in (p, p + 1, p + 2):
                        if q not in column:
                            column[q] = s[t, q, r + 1, here, :]
                    lower = (column[p], s[t, p + 1, r, here, :], s[t, p + 1, r + 1, z - 1:z + 7, :])
                    upper = (column[p + 2], s[t, p + 1, r + 2, here, :], s[t, p + 1, r + 1, z + 1:z + 9, :])
                    middle = column[p + 1]
                    value = middle
                    for k in range(3):
                        value = value - w[k, p, r, z - PAD:z - PAD + 8, :] * (upper[k] - lower[k])
                    spread = (lower[0] + upper[0]) + (lower[1] + upper[1]) + (lower[2] + upper[2])
                    value = value + 0.05 * (spread - 6.0 * middle)
                    if t == STEPS - 1:
                        out[p, r, z - PAD:z - PAD + 8, :] = value
                    else:
                        s[t + 1, p + 1, r + 1, here, :] = value
            return None

        lax.fori_loop(piece[0], piece[0] + piece[1], row, None)

    for t in range(STEPS - 1):
        wait_rest(t)
        sent = 0
        for i, piece in enumerate(parts[t]):
            if t == 0:
                wait_speeds(i)
            wait_py(t, i)
            update(t, piece, range(planes))
            while sent < len(parts[t + 1]) and sum(parts[t + 1][sent]) <= sum(piece):
                send_py(t + 1, sent)
                sent += 1
        send_rest(t + 1)

    last = STEPS - 1
    wait_rest(last)
    update(last, (0, rows), range(1, planes - 1))
    split = planes > 1 and counts["py"] > 1
    if split:
        for way in (0, 1):
            pl.when(jnp.logical_not(receives("py", way)))(
                lambda way=way: update(last, (0, rows), [(planes - 1) * way]))
    for t in range(last):
        wait_sent(t)
    for i, piece in enumerate(parts[last]):
        wait_py(last, i)
        if split:
            each("py", receives, lambda way: update(last, piece, [(planes - 1) * way]))
        else:
            update(last, piece, [p - 1 for p in outer])
    wait_sent(last)


def body(counts, x, vn, ve, vu):
    planes, rows, depth, lanes = x.shape
    most = max(len(pieces(rows, t)) for t in range(STEPS))
    dma = pltpu.SemaphoreType.DMA
    return pl.pallas_call(
        functools.partial(kernel, counts),
        out_shape=pltpu.VMEM(x.shape, x.dtype),
        in_specs=[pl.BlockSpec(memory_space=pl.ANY)] * 4,
        out_specs=pl.BlockSpec(memory_space=pltpu.VMEM),
        scratch_shapes=[
            pltpu.VMEM((STEPS, planes + 2, rows + 2, depth + 2 * PAD, lanes), x.dtype),
            pltpu.VMEM((3, planes, rows, depth, lanes), x.dtype),
            dma((2, most)),
            dma(()),
            dma((most,)),
            dma((2, STEPS)),
            dma((2, STEPS, most)),
            dma((2, STEPS)),
            dma((2, STEPS)),
            dma((2, STEPS)),
            dma((2, STEPS)),
        ],
        compiler_params=pltpu.CompilerParams(
            collective_id=0, has_side_effects=True, vmem_limit_bytes=54 * 2**20
        ),
    )(x, vn, ve, vu)


def solution(mesh):
    counts = {axis: mesh.shape[axis] for axis in ("py", "px", "pz")}
    spec = P(("site", "py"), "px", "pz", None)
    return jax.shard_map(
        functools.partial(body, counts), mesh=mesh, in_specs=(spec,) * 4, out_specs=spec,
        check_vma=False,
    )
```

profile of v0, /device:TPU:0, one launch (start us, length us, event | category | flops | bytes accessed | tf_op | source)
XLA Modules:
  0.0 97.6 jit_solution(8641882398383730744)
XLA Ops:
  0.0 95.6 %shard_map.46 = f32[4,64,32,128]{3,2,1,0:T(8,128)S(1)} custom-call(f32[4,64,32,128]{3,2,1,0:T(8,128)} %x.1, f32[4,64,32,128]{3,2,1,0:T(8,128)} %vn.1, f32[4,64,32,128]{3,2,1,0:T(8,128)} %ve.1, f32[4,64,32,128]{3,2,1,0:T(8,128)} %vu.1), custom_call_target="tpu_custom_call" | custom-call | tf_op jit(solution)/shard_map/pallas_call | solution.py:246
  95.6 2.0 %copy.6 = f32[4,64,32,128]{3,2,1,0:T(8,128)} copy(f32[4,64,32,128]{3,2,1,0:T(8,128)S(1)} %shard_map.46) | data formatting | bytes 8388608
where the time goes:
time: 97.7 us; the launch traced here: 97.6 us
  Pallas kernels  95.6 us (98%)
  local copies, waits for them, and re-layouts  2.02 us (2%)
    pallas_call x1, Pallas kernels, body(): pl.pallas_call(functools.partial(kernel, counts), out_shape=pltpu.VMEM(x....  95.6 us
    unnamed x1, local copies, waits for them, and re-layouts  2.02 us

commit v1 on v0

--- a/solution.py
+++ b/solution.py
@@ -11,6 +11,7 @@
 CUTS = ((0, 32, 64), (0, 32, 64), (0, 32, 64), (0, 32, 56, 62, 64))
 PAD = 8
 MESH = pl.DeviceIdType.MESH
+AXES = ("py", "px", "pz")
 
 
 def pieces(rows, t):
@@ -18,19 +19,23 @@
     return [(a, b - a) for a, b in zip(ends, ends[1:])]
 
 
+def most(rows, parity):
+    return max(len(pieces(rows, t)) for t in range(parity, STEPS, 2))
+
+
 def kernel(
     counts, x, vn, ve, vu, out, s, w,
     edge_sem, load_sem, speed_sem,
-    py_send, py_recv, px_send, px_recv, pz_send, pz_recv,
+    py_send, py_recv_even, py_recv_odd, px_send, px_recv, pz_send, pz_recv,
 ):
     planes, rows, depth, _ = x.shape
     parts = [pieces(rows, t) for t in range(STEPS)]
     cells = pl.ds(PAD, depth)
     speeds = (vn, ve, vu)
+    py_recv = (py_recv_even, py_recv_odd)
     outer = sorted({1, planes})
     inner_count = planes - 2
-    axes = ("py", "px", "pz")
-    index = {axis: lax.axis_index(axis) for axis in axes}
+    index = {axis: lax.axis_index(axis) for axis in AXES}
 
     def sends(axis, way):
         return index[axis] < counts[axis] - 1 if way == 0 else index[axis] > 0
@@ -41,6 +46,9 @@
     def target(axis, way):
         count = counts[axis]
         return {axis: lax.rem(index[axis] + (1 if way == 0 else count - 1), count)}
+
+    def lane(axis, way):
+        return way if counts[axis] > 2 else 0
 
     def remote(src, dst, send, recv, axis, way):
         return pltpu.make_async_remote_copy(
@@ -53,14 +61,14 @@
         here = pl.ds(1 + first, span)
         src = s.at[t, planes if way == 0 else 1, here, cells]
         dst = s.at[t, 0 if way == 0 else planes + 1, here, cells]
-        return remote(src, dst, py_send.at[way, t], py_recv.at[way, t, i], "py", way)
+        return remote(src, dst, py_send.at[lane("py", way)], py_recv[t % 2].at[lane("py", way), i], "py", way)
 
     def px_copy(way, t):
         row = rows if way == 0 else 1
         inner = pl.ds(1, planes)
         src = x.at[:, row - 1] if t == 0 else s.at[t, inner, row, cells]
         dst = s.at[t, inner, 0 if way == 0 else rows + 1, cells]
-        return remote(src, dst, px_send.at[way, t], px_recv.at[way, t], "px", way)
+        return remote(src, dst, px_send.at[lane("px", way)], px_recv.at[lane("px", way), t % 2], "px", way)
 
     def pz_copy(way, t):
         inner, here = pl.ds(1, planes), pl.ds(1, rows)
@@ -70,16 +78,17 @@
         else:
             src = s.at[t, inner, here, pl.ds(PAD + first, PAD)]
         dst = s.at[t, inner, here, pl.ds(0 if way == 0 else PAD + depth, PAD)]
-        return remote(src, dst, pz_send.at[way, t], pz_recv.at[way, t], "pz", way)
-
-    def wait_sent(t):
-        def py_wait(way):
-            block = s.at[t, planes if way == 0 else 1, pl.ds(1, rows), cells]
-            remote(block, block, py_send.at[way, t], py_recv.at[way, t, 0], "py", way).wait_send()
-
-        each("py", sends, py_wait)
-        each("pz", sends, lambda way: pz_copy(way, t).wait_send())
-        each("px", sends, lambda way: px_copy(way, t).wait_send())
+        return remote(src, dst, pz_send.at[lane("pz", way)], pz_recv.at[lane("pz", way), t % 2], "pz", way)
+
+    def wait_sent():
+        steps, inner, here = pl.ds(0, STEPS), pl.ds(1, planes), pl.ds(1, rows)
+
+        def wait(axis, sem, block, way):
+            pltpu.make_async_copy(block, block, sem.at[lane(axis, way)]).wait()
+
+        each("py", sends, functools.partial(wait, "py", py_send, s.at[steps, 1, here, cells]))
+        each("px", sends, functools.partial(wait, "px", px_send, s.at[steps, inner, 1, cells]))
+        each("pz", sends, functools.partial(wait, "pz", pz_send, s.at[steps, inner, here, pl.ds(PAD, PAD)]))
 
     def each(axis, test, action):
         if counts[axis] > 1:
@@ -118,7 +127,7 @@
 
     barrier = pltpu.get_barrier_semaphore()
     greeted = 0
-    for axis in axes:
+    for axis in AXES:
         each(axis, sends, lambda way, axis=axis: pl.semaphore_signal(
             barrier, inc=1, device_id=target(axis, way), device_id_type=MESH))
         if counts[axis] > 1:
@@ -175,7 +184,7 @@
 
         lax.fori_loop(0, STEPS, fill, None)
 
-    for axis in axes:
+    for axis in AXES:
         for way in (0, 1):
             pl.when(jnp.logical_not(receives(axis, way)))(functools.partial(clear, axis, way))
 
@@ -228,20 +237,19 @@
         for way in (0, 1):
             pl.when(jnp.logical_not(receives("py", way)))(
                 lambda way=way: update(last, (0, rows), [(planes - 1) * way]))
-    for t in range(last):
-        wait_sent(t)
     for i, piece in enumerate(parts[last]):
         wait_py(last, i)
         if split:
             each("py", receives, lambda way: update(last, piece, [(planes - 1) * way]))
         else:
             update(last, piece, [p - 1 for p in outer])
-    wait_sent(last)
+    wait_sent()
 
 
 def body(counts, x, vn, ve, vu):
     planes, rows, depth, lanes = x.shape
-    most = max(len(pieces(rows, t)) for t in range(STEPS))
+    first = len(pieces(rows, 0))
+    ways = {axis: 2 if counts[axis] > 2 else 1 for axis in AXES}
     dma = pltpu.SemaphoreType.DMA
     return pl.pallas_call(
         functools.partial(kernel, counts),
@@ -251,15 +259,16 @@
         scratch_shapes=[
             pltpu.VMEM((STEPS, planes + 2, rows + 2, depth + 2 * PAD, lanes), x.dtype),
             pltpu.VMEM((3, planes, rows, depth, lanes), x.dtype),
-            dma((2, most)),
+            dma((2, first)),
             dma(()),
-            dma((most,)),
-            dma((2, STEPS)),
-            dma((2, STEPS, most)),
-            dma((2, STEPS)),
-            dma((2, STEPS)),
-            dma((2, STEPS)),
-            dma((2, STEPS)),
+            dma((first,)),
+            dma((ways["py"],)),
+            dma((ways["py"], most(rows, 0))),
+            dma((ways["py"], most(rows, 1))),
+            dma((ways["px"],)),
+            dma((ways["px"], 2)),
+            dma((ways["pz"],)),
+            dma((ways["pz"], 2)),
         ],
         compiler_params=pltpu.CompilerParams(
             collective_id=0, has_side_effects=True, vmem_limit_bytes=54 * 2**20

time: 97.7 us -> 97.2 us (level)
  no operation moved by 1% of the time
where the time goes in v1:
time: 97.2 us; the launch traced here: 97 us
  Pallas kernels  95 us (98%)
  local copies, waits for them, and re-layouts  2.02 us (2%)
    pallas_call x1, Pallas kernels, body(): pl.pallas_call(functools.partial(kernel, counts), out_shape=pltpu.VMEM(x....  95 us
    unnamed x1, local copies, waits for them, and re-layouts  2.02 us

profile of v1, /device:TPU:0, one launch (start us, length us, event | category | flops | bytes accessed | tf_op | source)
XLA Modules:
  0.0 97.0 jit_solution(5137448622177600599)
XLA Ops:
  0.0 95.0 %shard_map.46 = f32[4,64,32,128]{3,2,1,0:T(8,128)S(1)} custom-call(f32[4,64,32,128]{3,2,1,0:T(8,128)} %x.1, f32[4,64,32,128]{3,2,1,0:T(8,128)} %vn.1, f32[4,64,32,128]{3,2,1,0:T(8,128)} %ve.1, f32[4,64,32,128]{3,2,1,0:T(8,128)} %vu.1), custom_call_target="tpu_custom_call" | custom-call | tf_op jit(solution)/shard_map/pallas_call | solution.py:254
  95.0 2.0 %copy.6 = f32[4,64,32,128]{3,2,1,0:T(8,128)} copy(f32[4,64,32,128]{3,2,1,0:T(8,128)S(1)} %shard_map.46) | data formatting | bytes 8388608

commit v2 on v1

--- a/solution.py
+++ b/solution.py
@@ -9,32 +9,33 @@
 
 STEPS = 4
 CUTS = ((0, 32, 64), (0, 32, 64), (0, 32, 64), (0, 32, 56, 62, 64))
+LOADS = (0, 4, 32, 64)
 PAD = 8
 MESH = pl.DeviceIdType.MESH
 AXES = ("py", "px", "pz")
 
 
-def pieces(rows, t):
-    ends = sorted({rows * cut // 64 for cut in CUTS[t]})
+def pieces(rows, cuts):
+    ends = sorted({rows * cut // 64 for cut in cuts})
     return [(a, b - a) for a, b in zip(ends, ends[1:])]
 
 
 def most(rows, parity):
-    return max(len(pieces(rows, t)) for t in range(parity, STEPS, 2))
+    return max(len(pieces(rows, CUTS[t])) for t in range(parity, STEPS, 2))
 
 
 def kernel(
     counts, x, vn, ve, vu, out, s, w,
-    edge_sem, load_sem, speed_sem,
+    hello, edge_sem, load_sem, speed_sem,
     py_send, py_recv_even, py_recv_odd, px_send, px_recv, pz_send, pz_recv,
 ):
     planes, rows, depth, _ = x.shape
-    parts = [pieces(rows, t) for t in range(STEPS)]
+    parts = [pieces(rows, CUTS[t]) for t in range(STEPS)]
+    loads = pieces(rows, LOADS)
     cells = pl.ds(PAD, depth)
     speeds = (vn, ve, vu)
     py_recv = (py_recv_even, py_recv_odd)
     outer = sorted({1, planes})
-    inner_count = planes - 2
     index = {axis: lax.axis_index(axis) for axis in AXES}
 
     def sends(axis, way):
@@ -56,8 +57,8 @@
             device_id=target(axis, way), device_id_type=MESH,
         )
 
-    def py_copy(way, t, i):
-        first, span = parts[t][i]
+    def py_copy(way, t, i, piece=None):
+        first, span = piece or parts[t][i]
         here = pl.ds(1 + first, span)
         src = s.at[t, planes if way == 0 else 1, here, cells]
         dst = s.at[t, 0 if way == 0 else planes + 1, here, cells]
@@ -98,6 +99,10 @@
     def send_py(t, i):
         each("py", sends, lambda way: py_copy(way, t, i).start())
 
+    def send_loaded(way, piece):
+        i = max(i for i, part in enumerate(parts[0]) if part[0] <= piece[0])
+        py_copy(way, 0, i, piece).start()
+
     def send_rest(t):
         each("px", sends, lambda way: px_copy(way, t).start())
         each("pz", sends, lambda way: pz_copy(way, t).start())
@@ -117,43 +122,76 @@
         block = w.at[:, :, pl.ds(*parts[0][i])]
         pltpu.make_async_copy(block, block, speed_sem.at[i]).wait()
 
-    def edge_load(k, i):
-        first, span = parts[0][i]
+    edge = jnp.where(sends("py", 0), planes, 1) if counts["py"] > 1 else planes
+
+    def edge_load(i):
+        first, span = loads[i]
         return pltpu.make_async_copy(
-            x.at[outer[k] - 1, pl.ds(first, span)],
-            s.at[0, outer[k], pl.ds(1 + first, span), cells],
-            edge_sem.at[k, i],
+            x.at[edge - 1, pl.ds(first, span)],
+            s.at[0, edge, pl.ds(1 + first, span), cells],
+            edge_sem.at[i],
         )
 
-    barrier = pltpu.get_barrier_semaphore()
-    greeted = 0
-    for axis in AXES:
-        each(axis, sends, lambda way, axis=axis: pl.semaphore_signal(
-            barrier, inc=1, device_id=target(axis, way), device_id_type=MESH))
-        if counts[axis] > 1:
-            for way in (0, 1):
-                greeted = greeted + sends(axis, way).astype(jnp.int32)
-    for i in range(len(parts[0])):
-        for k in range(len(outer)):
-            edge_load(k, i).start()
-    if inner_count > 0:
-        load = pltpu.make_async_copy(
-            x.at[pl.ds(1, inner_count)],
-            s.at[0, pl.ds(2, inner_count), pl.ds(1, rows), cells],
+    def rest_load():
+        first = jnp.where(edge == 1, 1, 0)
+        return pltpu.make_async_copy(
+            x.at[pl.ds(first, planes - 1)],
+            s.at[0, pl.ds(1 + first, planes - 1), pl.ds(1, rows), cells],
             load_sem,
         )
-        load.start()
+
+    def greet(axis, semaphore):
+        each(axis, sends, lambda way: pl.semaphore_signal(
+            semaphore, inc=1, device_id=target(axis, way), device_id_type=MESH))
+
+    def peers(axis):
+        if counts[axis] == 1:
+            return 0
+        return sum(sends(axis, way).astype(jnp.int32) for way in (0, 1))
+
+    def odd(axis):
+        return lax.rem(index[axis], 2) == 1
+
+    def even(axis):
+        return lax.rem(index[axis], 2) == 0
+
+    side = [axis for axis in ("px", "pz") if counts[axis] > 1]
+    barrier = pltpu.get_barrier_semaphore()
+    greet("py", barrier)
+    greeted = peers("py")
+    for axis in side:
+        pl.when(even(axis))(functools.partial(greet, axis, barrier))
+        greeted = greeted + lax.rem(index[axis], 2) * peers(axis)
+    for i in range(len(loads)):
+        edge_load(i).start()
+    if planes > 1:
+        rest_load().start()
+
+    both = jnp.logical_and(sends("py", 0), sends("py", 1)) if counts["py"] > 2 else jnp.bool_(False)
 
     pl.semaphore_wait(barrier, greeted)
 
-    for i in range(len(parts[0])):
-        for k in range(len(outer)):
-            edge_load(k, i).wait()
-        send_py(0, i)
-    send_rest(0)
+    for i, piece in enumerate(loads):
+        edge_load(i).wait()
+        if counts["py"] > 1:
+            pl.when(sends("py", 0))(lambda piece=piece: send_loaded(0, piece))
+            pl.when(jnp.logical_not(sends("py", 0)))(lambda piece=piece: send_loaded(1, piece))
+    if counts["py"] > 2:
+        @pl.when(both)
+        def _():
+            if planes > 1:
+                rest_load().wait()
+            for piece in loads:
+                send_loaded(1, piece)
+
+    for k, axis in enumerate(side):
+        pl.when(odd(axis))(functools.partial(greet, axis, hello.at[k]))
     for i in range(len(parts[0])):
         for k in range(3):
             speed_copy(k, i).start()
+    for k, axis in enumerate(side):
+        pl.when(even(axis))(lambda k=k, axis=axis: pl.semaphore_wait(hello.at[k], peers(axis)))
+    send_rest(0)
 
     def clear(axis, way):
         lanes = s.shape[-1]
@@ -188,8 +226,8 @@
         for way in (0, 1):
             pl.when(jnp.logical_not(receives(axis, way)))(functools.partial(clear, axis, way))
 
-    if inner_count > 0:
-        load.wait()
+    if planes > 1:
+        pl.when(jnp.logical_not(both))(lambda: rest_load().wait())
 
     def update(t, piece, wanted):
         def row(r, _):
@@ -248,7 +286,7 @@
 
 def body(counts, x, vn, ve, vu):
     planes, rows, depth, lanes = x.shape
-    first = len(pieces(rows, 0))
+    first = len(pieces(rows, CUTS[0]))
     ways = {axis: 2 if counts[axis] > 2 else 1 for axis in AXES}
     dma = pltpu.SemaphoreType.DMA
     return pl.pallas_call(
@@ -259,7 +297,8 @@
         scratch_shapes=[
             pltpu.VMEM((STEPS, planes + 2, rows + 2, depth + 2 * PAD, lanes), x.dtype),
             pltpu.VMEM((3, planes, rows, depth, lanes), x.dtype),
-            dma((2, first)),
+            pltpu.SemaphoreType.REGULAR((2,)),
+            dma((len(pieces(rows, LOADS)),)),
             dma(()),
             dma((first,)),
             dma((ways["py"],)),

time: 97.2 us -> 96.8 us (level)
  no operation moved by 1% of the time
where the time goes in v2:
time: 96.8 us; the launch traced here: 96.6 us
  Pallas kernels  94.6 us (98%)
  local copies, waits for them, and re-layouts  2.02 us (2%)
    pallas_call x1, Pallas kernels, body(): pl.pallas_call(functools.partial(kernel, counts), out_shape=pltpu.VMEM(x....  94.6 us
    unnamed x1, local copies, waits for them, and re-layouts  2.02 us

profile of v2, /device:TPU:0, one launch (start us, length us, event | category | flops | bytes accessed | tf_op | source)
XLA Modules:
  0.0 96.6 jit_solution(5954255338421594113)
XLA Ops:
  0.0 94.6 %shard_map.46 = f32[4,64,32,128]{3,2,1,0:T(8,128)S(1)} custom-call(f32[4,64,32,128]{3,2,1,0:T(8,128)} %x.1, f32[4,64,32,128]{3,2,1,0:T(8,128)} %vn.1, f32[4,64,32,128]{3,2,1,0:T(8,128)} %ve.1, f32[4,64,32,128]{3,2,1,0:T(8,128)} %vu.1), custom_call_target="tpu_custom_call" | custom-call | tf_op jit(solution)/shard_map/pallas_call | solution.py:292
  94.6 2.0 %copy.6 = f32[4,64,32,128]{3,2,1,0:T(8,128)} copy(f32[4,64,32,128]{3,2,1,0:T(8,128)S(1)} %shard_map.46) | data formatting | bytes 8388608

commit v3 on v2

--- a/solution.py
+++ b/solution.py
@@ -9,7 +9,7 @@
 
 STEPS = 4
 CUTS = ((0, 32, 64), (0, 32, 64), (0, 32, 64), (0, 32, 56, 62, 64))
-LOADS = (0, 4, 32, 64)
+LOADS = (0, 4, 32, 60, 64)
 PAD = 8
 MESH = pl.DeviceIdType.MESH
 AXES = ("py", "px", "pz")
@@ -25,9 +25,10 @@
 
 
 def kernel(
-    counts, x, vn, ve, vu, out, s, w,
+    counts, x, vn, ve, vu, out, s, w, via,
     hello, edge_sem, load_sem, speed_sem,
     py_send, py_recv_even, py_recv_odd, px_send, px_recv, pz_send, pz_recv,
+    pass_send, pass_recv,
 ):
     planes, rows, depth, _ = x.shape
     parts = [pieces(rows, CUTS[t]) for t in range(STEPS)]
@@ -62,7 +63,7 @@
         here = pl.ds(1 + first, span)
         src = s.at[t, planes if way == 0 else 1, here, cells]
         dst = s.at[t, 0 if way == 0 else planes + 1, here, cells]
-        return remote(src, dst, py_send.at[lane("py", way)], py_recv[t % 2].at[lane("py", way), i], "py", way)
+        return remote(src, dst, py_send.at[lane("py", way), min(t, 1)], py_recv[t % 2].at[lane("py", way), i], "py", way)
 
     def px_copy(way, t):
         row = rows if way == 0 else 1
@@ -82,33 +83,95 @@
         return remote(src, dst, pz_send.at[lane("pz", way)], pz_recv.at[lane("pz", way), t % 2], "pz", way)
 
     def wait_sent():
-        steps, inner, here = pl.ds(0, STEPS), pl.ds(1, planes), pl.ds(1, rows)
-
-        def wait(axis, sem, block, way):
-            pltpu.make_async_copy(block, block, sem.at[lane(axis, way)]).wait()
-
-        each("py", sends, functools.partial(wait, "py", py_send, s.at[steps, 1, here, cells]))
-        each("px", sends, functools.partial(wait, "px", px_send, s.at[steps, inner, 1, cells]))
-        each("pz", sends, functools.partial(wait, "pz", pz_send, s.at[steps, inner, here, pl.ds(PAD, PAD)]))
+        inner, here = pl.ds(1, planes), pl.ds(1, rows)
+        every, later = pl.ds(0, STEPS), pl.ds(1, STEPS - 1)
+
+        def wait(semaphore, block):
+            pltpu.make_async_copy(block, block, semaphore).wait()
+
+        def py_wait(way):
+            def first_wait(span):
+                wait(py_send.at[lane("py", way), 0], s.at[0, 1, pl.ds(1, span), cells])
+
+            by_relay(way, lambda: first_wait(chunk[0]), lambda: first_wait(rows))
+            wait(py_send.at[lane("py", way), 1], s.at[later, 1, here, cells])
+
+        each("py", sends, py_wait)
+        each("px", sends, lambda way: wait(px_send.at[lane("px", way)], s.at[every, inner, 1, cells]))
+        each("pz", sends, lambda way: wait(
+            pz_send.at[lane("pz", way)], s.at[every, inner, here, pl.ds(PAD, PAD)]))
+        if relayed:
+            pl.when(jnp.logical_or(hands, relays))(lambda: hop_in().wait_send())
 
     def each(axis, test, action):
         if counts[axis] > 1:
             for way in (0, 1):
                 pl.when(test(axis, way))(functools.partial(action, way))
 
+    def odd(axis):
+        return lax.rem(index[axis], 2) == 1
+
+    def even(axis):
+        return lax.rem(index[axis], 2) == 0
+
+    chunk = loads[-1]
+    relayed = counts["py"] > 1 and counts["px"] > 1
+    if relayed:
+        front = index["pz"] == 0
+        paired = jnp.logical_and(front, jnp.logical_and(even("px"), sends("px", 0)))
+        hands = jnp.logical_and(paired, sends("py", 1))
+        relays = jnp.logical_and(jnp.logical_and(front, odd("px")), sends("py", 1))
+
+    def by_relay(way, yes, no):
+        if relayed and way == 1:
+            pl.when(paired)(yes)
+            pl.when(jnp.logical_not(paired))(no)
+        else:
+            no()
+
+    def hop(src, dst, device):
+        return pltpu.make_async_remote_copy(
+            src_ref=src, dst_ref=dst, send_sem=pass_send, recv_sem=pass_recv,
+            device_id=device, device_id_type=MESH,
+        )
+
+    def hop_in():
+        return hop(s.at[0, 1, pl.ds(1 + chunk[0], chunk[1]), cells], via, target("px", 0))
+
+    def hop_out():
+        landing = s.at[0, planes + 1, pl.ds(1 + chunk[0], chunk[1]), cells]
+        return hop(via, landing, {**target("py", 1), **target("px", 1)})
+
     def send_py(t, i):
         each("py", sends, lambda way: py_copy(way, t, i).start())
 
     def send_loaded(way, piece):
         i = max(i for i, part in enumerate(parts[0]) if part[0] <= piece[0])
-        py_copy(way, 0, i, piece).start()
+        start = lambda: py_copy(way, 0, i, piece).start()
+        if piece == chunk:
+            by_relay(way, lambda: None, start)
+        else:
+            start()
 
     def send_rest(t):
         each("px", sends, lambda way: px_copy(way, t).start())
         each("pz", sends, lambda way: pz_copy(way, t).start())
 
     def wait_py(t, i):
-        each("py", receives, lambda way: py_copy(way, t, i).wait_recv())
+        def wait(way):
+            whole = lambda: py_copy(way, t, i).wait_recv()
+
+            def split():
+                first = parts[0][i][0]
+                py_copy(way, 0, i, (first, chunk[0] - first)).wait_recv()
+                hop_out().wait_recv()
+
+            if t == 0 and sum(parts[0][i]) == rows:
+                by_relay(way, split, whole)
+            else:
+                whole()
+
+        each("py", receives, wait)
 
     def wait_rest(t):
         each("px", receives, lambda way: px_copy(way, t).wait_recv())
@@ -148,12 +211,6 @@
         if counts[axis] == 1:
             return 0
         return sum(sends(axis, way).astype(jnp.int32) for way in (0, 1))
-
-    def odd(axis):
-        return lax.rem(index[axis], 2) == 1
-
-    def even(axis):
-        return lax.rem(index[axis], 2) == 0
 
     side = [axis for axis in ("px", "pz") if counts[axis] > 1]
     barrier = pltpu.get_barrier_semaphore()
@@ -191,6 +248,8 @@
             speed_copy(k, i).start()
     for k, axis in enumerate(side):
         pl.when(even(axis))(lambda k=k, axis=axis: pl.semaphore_wait(hello.at[k], peers(axis)))
+    if relayed:
+        pl.when(hands)(lambda: hop_in().start())
     send_rest(0)
 
     def clear(axis, way):
@@ -228,6 +287,12 @@
 
     if planes > 1:
         pl.when(jnp.logical_not(both))(lambda: rest_load().wait())
+
+    if relayed:
+        @pl.when(relays)
+        def _():
+            hop_in().wait_recv()
+            hop_out().start()
 
     def update(t, piece, wanted):
         def row(r, _):
@@ -297,17 +362,20 @@
         scratch_shapes=[
             pltpu.VMEM((STEPS, planes + 2, rows + 2, depth + 2 * PAD, lanes), x.dtype),
             pltpu.VMEM((3, planes, rows, depth, lanes), x.dtype),
+            pltpu.VMEM((pieces(rows, LOADS)[-1][1], depth, lanes), x.dtype),
             pltpu.SemaphoreType.REGULAR((2,)),
             dma((len(pieces(rows, LOADS)),)),
             dma(()),
             dma((first,)),
-            dma((ways["py"],)),
+            dma((ways["py"], 2)),
             dma((ways["py"], most(rows, 0))),
             dma((ways["py"], most(rows, 1))),
             dma((ways["px"],)),
             dma((ways["px"], 2)),
             dma((ways["pz"],)),
             dma((ways["pz"], 2)),
+            dma(()),
+            dma(()),
         ],
         compiler_params=pltpu.CompilerParams(
             collective_id=0, has_side_effects=True, vmem_limit_bytes=54 * 2**20

time: 96.8 us -> 96.1 us (level)
  no operation moved by 1% of the time
where the time goes in v3:
time: 96.1 us; the launch traced here: 96 us
  Pallas kernels  93.9 us (98%)
  local copies, waits for them, and re-layouts  2.02 us (2%)
    pallas_call x1, Pallas kernels, body(): pl.pallas_call(functools.partial(kernel, counts), out_shape=pltpu.VMEM(x....  93.9 us
    unnamed x1, local copies, waits for them, and re-layouts  2.02 us

profile of v3, /device:TPU:0, one launch (start us, length us, event | category | flops | bytes accessed | tf_op | source)
XLA Modules:
  0.0 96.0 jit_solution(14024974854656446110)
XLA Ops:
  0.0 93.9 %shard_map.46 = f32[4,64,32,128]{3,2,1,0:T(8,128)S(1)} custom-call(f32[4,64,32,128]{3,2,1,0:T(8,128)} %x.1, f32[4,64,32,128]{3,2,1,0:T(8,128)} %vn.1, f32[4,64,32,128]{3,2,1,0:T(8,128)} %ve.1, f32[4,64,32,128]{3,2,1,0:T(8,128)} %vu.1), custom_call_target="tpu_custom_call" | custom-call | tf_op jit(solution)/shard_map/pallas_call | solution.py:357
  93.9 2.0 %copy.6 = f32[4,64,32,128]{3,2,1,0:T(8,128)} copy(f32[4,64,32,128]{3,2,1,0:T(8,128)S(1)} %shard_map.46) | data formatting | bytes 8388608

commit v4 on v3

--- a/solution.py
+++ b/solution.py
@@ -9,7 +9,8 @@
 
 STEPS = 4
 CUTS = ((0, 32, 64), (0, 32, 64), (0, 32, 64), (0, 32, 56, 62, 64))
-LOADS = (0, 4, 32, 60, 64)
+LOADS = (0, 4, 32, 58, 64)
+ROUTES = 3
 PAD = 8
 MESH = pl.DeviceIdType.MESH
 AXES = ("py", "px", "pz")
@@ -22,6 +23,10 @@
 
 def most(rows, parity):
     return max(len(pieces(rows, CUTS[t])) for t in range(parity, STEPS, 2))
+
+
+def detours(counts):
+    return min(ROUTES, counts["site"] - 1) if counts["py"] > 1 else 0
 
 
 def kernel(
@@ -37,7 +42,7 @@
     speeds = (vn, ve, vu)
     py_recv = (py_recv_even, py_recv_odd)
     outer = sorted({1, planes})
-    index = {axis: lax.axis_index(axis) for axis in AXES}
+    index = {axis: lax.axis_index(axis) for axis in (*AXES, "site")}
 
     def sends(axis, way):
         return index[axis] < counts[axis] - 1 if way == 0 else index[axis] > 0
@@ -93,15 +98,17 @@
             def first_wait(span):
                 wait(py_send.at[lane("py", way), 0], s.at[0, 1, pl.ds(1, span), cells])
 
-            by_relay(way, lambda: first_wait(chunk[0]), lambda: first_wait(rows))
+            by_route(way, lambda: first_wait(rows), lambda: first_wait(chunk[0]))
             wait(py_send.at[lane("py", way), 1], s.at[later, 1, here, cells])
 
         each("py", sends, py_wait)
         each("px", sends, lambda way: wait(px_send.at[lane("px", way)], s.at[every, inner, 1, cells]))
         each("pz", sends, lambda way: wait(
             pz_send.at[lane("pz", way)], s.at[every, inner, here, pl.ds(PAD, PAD)]))
-        if relayed:
-            pl.when(jnp.logical_or(hands, relays))(lambda: hop_in().wait_send())
+        if routes:
+            pl.when(hands)(lambda: wait(pass_send, s.at[0, 1, pl.ds(1, chunk[1]), cells]))
+        for k in range(routes):
+            pl.when(relays[k])(lambda k=k: hop_out(k).wait_send())
 
     def each(axis, test, action):
         if counts[axis] > 1:
@@ -114,33 +121,40 @@
     def even(axis):
         return lax.rem(index[axis], 2) == 0
 
-    chunk = loads[-1]
-    relayed = counts["py"] > 1 and counts["px"] > 1
-    if relayed:
-        front = index["pz"] == 0
-        paired = jnp.logical_and(front, jnp.logical_and(even("px"), sends("px", 0)))
-        hands = jnp.logical_and(paired, sends("py", 1))
-        relays = jnp.logical_and(jnp.logical_and(front, odd("px")), sends("py", 1))
-
-    def by_relay(way, yes, no):
-        if relayed and way == 1:
-            pl.when(paired)(yes)
-            pl.when(jnp.logical_not(paired))(no)
-        else:
-            no()
-
-    def hop(src, dst, device):
+    chunk, routes = loads[-1], detours(counts)
+    front = jnp.logical_and(index["pz"] == 0, even("px"))
+    late = jnp.logical_and(front, index["site"] == 0)
+    hands = jnp.logical_and(late, sends("py", 1))
+    takes = jnp.logical_and(late, receives("py", 1))
+    twin = jnp.logical_and(front, receives("py", 1))
+    relays = [jnp.logical_and(twin, index["site"] == k + 1) for k in range(routes)]
+
+    def part(k):
+        ends = [chunk[0] + chunk[1] * j // routes for j in (k, k + 1)]
+        return ends[0], ends[1] - ends[0]
+
+    def hop(k, src, dst, device):
         return pltpu.make_async_remote_copy(
-            src_ref=src, dst_ref=dst, send_sem=pass_send, recv_sem=pass_recv,
+            src_ref=src, dst_ref=dst, send_sem=pass_send, recv_sem=pass_recv.at[k],
             device_id=device, device_id_type=MESH,
         )
 
-    def hop_in():
-        return hop(s.at[0, 1, pl.ds(1 + chunk[0], chunk[1]), cells], via, target("px", 0))
-
-    def hop_out():
-        landing = s.at[0, planes + 1, pl.ds(1 + chunk[0], chunk[1]), cells]
-        return hop(via, landing, {**target("py", 1), **target("px", 1)})
+    def hop_in(k):
+        first, span = part(k)
+        src = s.at[0, 1, pl.ds(1 + first, span), cells]
+        return hop(k, src, via.at[pl.ds(0, span)], {**target("py", 1), "site": k + 1})
+
+    def hop_out(k):
+        first, span = part(k)
+        dst = s.at[0, planes + 1, pl.ds(1 + first, span), cells]
+        return hop(k, via.at[pl.ds(0, span)], dst, {"site": 0})
+
+    def by_route(way, straight, split):
+        if way == 1 and routes:
+            pl.when(late)(split)
+            pl.when(jnp.logical_not(late))(straight)
+        else:
+            straight()
 
     def send_py(t, i):
         each("py", sends, lambda way: py_copy(way, t, i).start())
@@ -149,7 +163,7 @@
         i = max(i for i, part in enumerate(parts[0]) if part[0] <= piece[0])
         start = lambda: py_copy(way, 0, i, piece).start()
         if piece == chunk:
-            by_relay(way, lambda: None, start)
+            by_route(way, start, lambda: None)
         else:
             start()
 
@@ -159,15 +173,17 @@
 
     def wait_py(t, i):
         def wait(way):
-            whole = lambda: py_copy(way, t, i).wait_recv()
+            def whole():
+                py_copy(way, t, i).wait_recv()
 
             def split():
                 first = parts[0][i][0]
                 py_copy(way, 0, i, (first, chunk[0] - first)).wait_recv()
-                hop_out().wait_recv()
+                for k in range(routes):
+                    hop_out(k).wait_recv()
 
             if t == 0 and sum(parts[0][i]) == rows:
-                by_relay(way, split, whole)
+                by_route(way, whole, split)
             else:
                 whole()
 
@@ -219,6 +235,10 @@
     for axis in side:
         pl.when(even(axis))(functools.partial(greet, axis, barrier))
         greeted = greeted + lax.rem(index[axis], 2) * peers(axis)
+    for k in range(routes):
+        pl.when(takes)(lambda k=k: pl.semaphore_signal(
+            barrier, inc=1, device_id={"site": k + 1}, device_id_type=MESH))
+        greeted = greeted + relays[k].astype(jnp.int32)
     for i in range(len(loads)):
         edge_load(i).start()
     if planes > 1:
@@ -243,13 +263,27 @@
 
     for k, axis in enumerate(side):
         pl.when(odd(axis))(functools.partial(greet, axis, hello.at[k]))
+    for k in range(routes):
+        pl.when(relays[k])(lambda: pl.semaphore_signal(
+            hello.at[2], inc=1, device_id={"site": 0}, device_id_type=MESH))
     for i in range(len(parts[0])):
         for k in range(3):
             speed_copy(k, i).start()
     for k, axis in enumerate(side):
         pl.when(even(axis))(lambda k=k, axis=axis: pl.semaphore_wait(hello.at[k], peers(axis)))
-    if relayed:
-        pl.when(hands)(lambda: hop_in().start())
+    if routes:
+        @pl.when(takes)
+        def _():
+            pl.semaphore_wait(hello.at[2], routes)
+            pl.semaphore_signal(
+                hello.at[3], inc=1, device_id=target("py", 0), device_id_type=MESH)
+
+        @pl.when(hands)
+        def _():
+            pl.semaphore_wait(hello.at[3], 1)
+            for k in range(routes):
+                hop_in(k).start()
+
     send_rest(0)
 
     def clear(axis, way):
@@ -288,11 +322,11 @@
     if planes > 1:
         pl.when(jnp.logical_not(both))(lambda: rest_load().wait())
 
-    if relayed:
-        @pl.when(relays)
-        def _():
-            hop_in().wait_recv()
-            hop_out().start()
+    for k in range(routes):
+        @pl.when(relays[k])
+        def _(k=k):
+            hop_in(k).wait_recv()
+            hop_out(k).start()
 
     def update(t, piece, wanted):
         def row(r, _):
@@ -363,7 +397,7 @@
             pltpu.VMEM((STEPS, planes + 2, rows + 2, depth + 2 * PAD, lanes), x.dtype),
             pltpu.VMEM((3, planes, rows, depth, lanes), x.dtype),
             pltpu.VMEM((pieces(rows, LOADS)[-1][1], depth, lanes), x.dtype),
-            pltpu.SemaphoreType.REGULAR((2,)),
+            pltpu.SemaphoreType.REGULAR((4,)),
             dma((len(pieces(rows, LOADS)),)),
             dma(()),
             dma((first,)),
@@ -375,7 +409,7 @@
             dma((ways["pz"],)),
             dma((ways["pz"], 2)),
             dma(()),
-            dma(()),
+            dma((max(detours(counts), 1),)),
         ],
         compiler_params=pltpu.CompilerParams(
             collective_id=0, has_side_effects=True, vmem_limit_bytes=54 * 2**20
@@ -384,7 +418,7 @@
 
 
 def solution(mesh):
-    counts = {axis: mesh.shape[axis] for axis in ("py", "px", "pz")}
+    counts = {axis: mesh.shape[axis] for axis in (*AXES, "site")}
     spec = P(("site", "py"), "px", "pz", None)
     return jax.shard_map(
         functools.partial(body, counts), mesh=mesh, in_specs=(spec,) * 4, out_specs=spec,

time: 96.1 us -> 95.7 us (level)
  no operation moved by 1% of the time
where the time goes in v4:
time: 95.7 us; the launch traced here: 95.4 us
  Pallas kernels  93.4 us (98%)
  local copies, waits for them, and re-layouts  2.02 us (2%)
    pallas_call x1, Pallas kernels, body(): pl.pallas_call(functools.partial(kernel, counts), out_shape=pltpu.VMEM(x....  93.4 us
    unnamed x1, local copies, waits for them, and re-layouts  2.02 us

profile of v4, /device:TPU:0, one launch (start us, length us, event | category | flops | bytes accessed | tf_op | source)
XLA Modules:
  0.0 95.4 jit_solution(12391801622300947155)
XLA Ops:
  0.0 93.4 %shard_map.46 = f32[4,64,32,128]{3,2,1,0:T(8,128)S(1)} custom-call(f32[4,64,32,128]{3,2,1,0:T(8,128)} %x.1, f32[4,64,32,128]{3,2,1,0:T(8,128)} %vn.1, f32[4,64,32,128]{3,2,1,0:T(8,128)} %ve.1, f32[4,64,32,128]{3,2,1,0:T(8,128)} %vu.1), custom_call_target="tpu_custom_call" | custom-call | tf_op jit(solution)/shard_map/pallas_call | solution.py:391
  93.4 2.0 %copy.6 = f32[4,64,32,128]{3,2,1,0:T(8,128)} copy(f32[4,64,32,128]{3,2,1,0:T(8,128)S(1)} %shard_map.46) | data formatting | bytes 8388608

commit v5 on v4

--- a/solution.py
+++ b/solution.py
@@ -31,7 +31,7 @@
 
 def kernel(
     counts, x, vn, ve, vu, out, s, w, via,
-    hello, edge_sem, load_sem, speed_sem,
+    hello, edge_sem, load_sem,
     py_send, py_recv_even, py_recv_odd, px_send, px_recv, pz_send, pz_recv,
     pass_send, pass_recv,
 ):
@@ -133,21 +133,21 @@
         ends = [chunk[0] + chunk[1] * j // routes for j in (k, k + 1)]
         return ends[0], ends[1] - ends[0]
 
-    def hop(k, src, dst, device):
+    def hop(src, dst, device):
         return pltpu.make_async_remote_copy(
-            src_ref=src, dst_ref=dst, send_sem=pass_send, recv_sem=pass_recv.at[k],
+            src_ref=src, dst_ref=dst, send_sem=pass_send, recv_sem=pass_recv,
             device_id=device, device_id_type=MESH,
         )
 
     def hop_in(k):
         first, span = part(k)
         src = s.at[0, 1, pl.ds(1 + first, span), cells]
-        return hop(k, src, via.at[pl.ds(0, span)], {**target("py", 1), "site": k + 1})
+        return hop(src, via.at[pl.ds(0, span)], {**target("py", 1), "site": k + 1})
 
     def hop_out(k):
         first, span = part(k)
         dst = s.at[0, planes + 1, pl.ds(1 + first, span), cells]
-        return hop(k, via.at[pl.ds(0, span)], dst, {"site": 0})
+        return hop(via.at[pl.ds(0, span)], dst, {"site": 0})
 
     def by_route(way, straight, split):
         if way == 1 and routes:
@@ -179,8 +179,8 @@
             def split():
                 first = parts[0][i][0]
                 py_copy(way, 0, i, (first, chunk[0] - first)).wait_recv()
-                for k in range(routes):
-                    hop_out(k).wait_recv()
+                block = s.at[0, planes + 1, pl.ds(1 + chunk[0], chunk[1]), cells]
+                pltpu.make_async_copy(block, block, pass_recv).wait()
 
             if t == 0 and sum(parts[0][i]) == rows:
                 by_route(way, whole, split)
@@ -195,11 +195,11 @@
 
     def speed_copy(k, i):
         here = pl.ds(*parts[0][i])
-        return pltpu.make_async_copy(speeds[k].at[:, here], w.at[k, :, here], speed_sem.at[i])
+        return pltpu.make_async_copy(speeds[k].at[:, here], w.at[k, :, here], edge_sem.at[i])
 
     def wait_speeds(i):
         block = w.at[:, :, pl.ds(*parts[0][i])]
-        pltpu.make_async_copy(block, block, speed_sem.at[i]).wait()
+        pltpu.make_async_copy(block, block, edge_sem.at[i]).wait()
 
     edge = jnp.where(sends("py", 0), planes, 1) if counts["py"] > 1 else planes
 
@@ -227,6 +227,11 @@
         if counts[axis] == 1:
             return 0
         return sum(sends(axis, way).astype(jnp.int32) for way in (0, 1))
+
+    for i in range(len(loads)):
+        edge_load(i).start()
+    if planes > 1:
+        rest_load().start()
 
     side = [axis for axis in ("px", "pz") if counts[axis] > 1]
     barrier = pltpu.get_barrier_semaphore()
@@ -239,11 +244,6 @@
         pl.when(takes)(lambda k=k: pl.semaphore_signal(
             barrier, inc=1, device_id={"site": k + 1}, device_id_type=MESH))
         greeted = greeted + relays[k].astype(jnp.int32)
-    for i in range(len(loads)):
-        edge_load(i).start()
-    if planes > 1:
-        rest_load().start()
-
     both = jnp.logical_and(sends("py", 0), sends("py", 1)) if counts["py"] > 2 else jnp.bool_(False)
 
     pl.semaphore_wait(barrier, greeted)
@@ -261,26 +261,27 @@
             for piece in loads:
                 send_loaded(1, piece)
 
-    for k, axis in enumerate(side):
-        pl.when(odd(axis))(functools.partial(greet, axis, hello.at[k]))
+    for axis in side:
+        pl.when(odd(axis))(functools.partial(greet, axis, hello.at[0]))
     for k in range(routes):
         pl.when(relays[k])(lambda: pl.semaphore_signal(
-            hello.at[2], inc=1, device_id={"site": 0}, device_id_type=MESH))
+            hello.at[0], inc=1, device_id={"site": 0}, device_id_type=MESH))
     for i in range(len(parts[0])):
         for k in range(3):
             speed_copy(k, i).start()
-    for k, axis in enumerate(side):
-        pl.when(even(axis))(lambda k=k, axis=axis: pl.semaphore_wait(hello.at[k], peers(axis)))
+    answers = sum((1 - lax.rem(index[axis], 2)) * peers(axis) for axis in side)
+    answers = answers + routes * takes.astype(jnp.int32)
+    if side or routes:
+        pl.when(answers > 0)(lambda: pl.semaphore_wait(hello.at[0], answers))
     if routes:
         @pl.when(takes)
         def _():
-            pl.semaphore_wait(hello.at[2], routes)
             pl.semaphore_signal(
-                hello.at[3], inc=1, device_id=target("py", 0), device_id_type=MESH)
+                hello.at[1], inc=1, device_id=target("py", 0), device_id_type=MESH)
 
         @pl.when(hands)
         def _():
-            pl.semaphore_wait(hello.at[3], 1)
+            pl.semaphore_wait(hello.at[1], 1)
             for k in range(routes):
                 hop_in(k).start()
 
@@ -385,7 +386,6 @@
 
 def body(counts, x, vn, ve, vu):
     planes, rows, depth, lanes = x.shape
-    first = len(pieces(rows, CUTS[0]))
     ways = {axis: 2 if counts[axis] > 2 else 1 for axis in AXES}
     dma = pltpu.SemaphoreType.DMA
     return pl.pallas_call(
@@ -397,10 +397,9 @@
             pltpu.VMEM((STEPS, planes + 2, rows + 2, depth + 2 * PAD, lanes), x.dtype),
             pltpu.VMEM((3, planes, rows, depth, lanes), x.dtype),
             pltpu.VMEM((pieces(rows, LOADS)[-1][1], depth, lanes), x.dtype),
-            pltpu.SemaphoreType.REGULAR((4,)),
-            dma((len(pieces(rows, LOADS)),)),
+            pltpu.SemaphoreType.REGULAR((2,)),
+            dma((max(len(pieces(rows, LOADS)), len(pieces(rows, CUTS[0]))),)),
             dma(()),
-            dma((first,)),
             dma((ways["py"], 2)),
             dma((ways["py"], most(rows, 0))),
             dma((ways["py"], most(rows, 1))),
@@ -409,7 +408,7 @@
             dma((ways["pz"],)),
             dma((ways["pz"], 2)),
             dma(()),
-            dma((max(detours(counts), 1),)),
+            dma(()),
         ],
         compiler_params=pltpu.CompilerParams(
             collective_id=0, has_side_effects=True, vmem_limit_bytes=54 * 2**20

time: 95.7 us -> 95.7 us (level)
  no operation moved by 1% of the time
where the time goes in v5:
time: 95.7 us; the launch traced here: 95.4 us
  Pallas kernels  93.4 us (98%)
  local copies, waits for them, and re-layouts  2.02 us (2%)
    pallas_call x1, Pallas kernels, body(): pl.pallas_call(functools.partial(kernel, counts), out_shape=pltpu.VMEM(x....  93.4 us
    unnamed x1, local copies, waits for them, and re-layouts  2.02 us

profile of v5, /device:TPU:0, one launch (start us, length us, event | category | flops | bytes accessed | tf_op | source)
XLA Modules:
  0.0 95.4 jit_solution(1841106514935384163)
XLA Ops:
  0.0 93.4 %shard_map.46 = f32[4,64,32,128]{3,2,1,0:T(8,128)S(1)} custom-call(f32[4,64,32,128]{3,2,1,0:T(8,128)} %x.1, f32[4,64,32,128]{3,2,1,0:T(8,128)} %vn.1, f32[4,64,32,128]{3,2,1,0:T(8,128)} %ve.1, f32[4,64,32,128]{3,2,1,0:T(8,128)} %vu.1), custom_call_target="tpu_custom_call" | custom-call | tf_op jit(solution)/shard_map/pallas_call | solution.py:391
  93.4 2.0 %copy.6 = f32[4,64,32,128]{3,2,1,0:T(8,128)} copy(f32[4,64,32,128]{3,2,1,0:T(8,128)S(1)} %shard_map.46) | data formatting | bytes 8388608

commit v6 on v5

--- a/solution.py
+++ b/solution.py
@@ -8,7 +8,7 @@
 from jax.sharding import PartitionSpec as P
 
 STEPS = 4
-CUTS = ((0, 32, 64), (0, 32, 64), (0, 32, 64), (0, 32, 56, 62, 64))
+CUTS = ((0, 32, 64), (0, 32, 64), (0, 32, 64), (0, 32, 52, 60, 63, 64))
 LOADS = (0, 4, 32, 58, 64)
 ROUTES = 3
 PAD = 8

time: 95.7 us -> 95.7 us (level)
  no operation moved by 1% of the time
where the time goes in v6:
time: 95.7 us; the launch traced here: 95.4 us
  Pallas kernels  93.4 us (98%)
  local copies, waits for them, and re-layouts  2.02 us (2%)
    pallas_call x1, Pallas kernels, body(): pl.pallas_call(functools.partial(kernel, counts), out_shape=pltpu.VMEM(x....  93.4 us
    unnamed x1, local copies, waits for them, and re-layouts  2.02 us

profile of v6, /device:TPU:0, one launch (start us, length us, event | category | flops | bytes accessed | tf_op | source)
XLA Modules:
  0.0 95.4 jit_solution(15397861068259195899)
XLA Ops:
  0.0 93.4 %shard_map.46 = f32[4,64,32,128]{3,2,1,0:T(8,128)S(1)} custom-call(f32[4,64,32,128]{3,2,1,0:T(8,128)} %x.1, f32[4,64,32,128]{3,2,1,0:T(8,128)} %vn.1, f32[4,64,32,128]{3,2,1,0:T(8,128)} %ve.1, f32[4,64,32,128]{3,2,1,0:T(8,128)} %vu.1), custom_call_target="tpu_custom_call" | custom-call | tf_op jit(solution)/shard_map/pallas_call | solution.py:391
  93.4 2.0 %copy.6 = f32[4,64,32,128]{3,2,1,0:T(8,128)} copy(f32[4,64,32,128]{3,2,1,0:T(8,128)S(1)} %shard_map.46) | data formatting | bytes 8388608

commit v7 on v6

--- a/solution.py
+++ b/solution.py
@@ -9,7 +9,7 @@
 
 STEPS = 4
 CUTS = ((0, 32, 64), (0, 32, 64), (0, 32, 64), (0, 32, 52, 60, 63, 64))
-LOADS = (0, 4, 32, 58, 64)
+LOADS = (0, 2, 32, 58, 64)
 ROUTES = 3
 PAD = 8
 MESH = pl.DeviceIdType.MESH

time: 95.7 us -> 95.6 us (level)
  no operation moved by 1% of the time
where the time goes in v7:
time: 95.6 us; the launch traced here: 95.3 us
  Pallas kernels  93.3 us (98%)
  local copies, waits for them, and re-layouts  2.02 us (2%)
    pallas_call x1, Pallas kernels, body(): pl.pallas_call(functools.partial(kernel, counts), out_shape=pltpu.VMEM(x....  93.3 us
    unnamed x1, local copies, waits for them, and re-layouts  2.02 us

profile of v7, /device:TPU:0, one launch (start us, length us, event | category | flops | bytes accessed | tf_op | source)
XLA Modules:
  0.0 95.3 jit_solution(16743376048481087273)
XLA Ops:
  0.0 93.3 %shard_map.46 = f32[4,64,32,128]{3,2,1,0:T(8,128)S(1)} custom-call(f32[4,64,32,128]{3,2,1,0:T(8,128)} %x.1, f32[4,64,32,128]{3,2,1,0:T(8,128)} %vn.1, f32[4,64,32,128]{3,2,1,0:T(8,128)} %ve.1, f32[4,64,32,128]{3,2,1,0:T(8,128)} %vu.1), custom_call_target="tpu_custom_call" | custom-call | tf_op jit(solution)/shard_map/pallas_call | solution.py:391
  93.3 2.0 %copy.6 = f32[4,64,32,128]{3,2,1,0:T(8,128)} copy(f32[4,64,32,128]{3,2,1,0:T(8,128)S(1)} %shard_map.46) | data formatting | bytes 8388608
